TPU v7x, 32 devices: a whole 2x2x4 slice. The times are simulated.
32 devices in a mesh: sub: 8 (over z, y), grp: 4 (over x, core).
Axes of the slice: x: 2, y: 2, z: 4, core: 2. Of those that a mesh axis runs over, the one named last changes fastest.
Arguments:
- rr_inverse: float32 [64, 512, 512], P(('sub', 'grp')), may hold values from -4 to 4, as said below
- corner_modes: float32 [64, 64, 512], P(('sub', 'grp')), may hold values from -0.5 to 0.5
- coarse_inverse: float32 [2048, 2048], P(('sub', 'grp')), may hold values from -1 to 1, as said below
- inertia: float32 [64, 512], P(('sub', 'grp')), may hold values from 0.5 to 2
- disp_now: float32 [8, 64, 512], P(None, ('sub', 'grp')), may hold values from -4 to 4
- vel_now: float32 [8, 64, 512], P(None, ('sub', 'grp')), may hold values from -4 to 4
- acc_now: float32 [8, 64, 512], P(None, ('sub', 'grp')), may hold values from -8 to 8
- load_next: float32 [8, 64, 512], P(None, ('sub', 'grp')), may hold values from -10 to 10
- basis_rows: float32 [32768, 256], P(('sub', 'grp')), may hold values from -0.03125 to 0.03125
- piece_owner: int32 [32], replicated, may hold values from 0 to 31, each once
Outputs:
- disp_new: float32 [8, 64, 512], P(None, ('sub', 'grp'))
- vel_new: float32 [8, 64, 512], P(None, ('sub', 'grp'))
- projection: float32 [256, 8], replicated
- r_factor: float32 [8, 8], replicated
- new_columns: float32 [8, 32768], P(None, ('sub', 'grp'))
Inputs may be any that keep to these rules, and one draw needn't show every extreme that they name: piece_owner is a permutation. `rr_inverse`: each of the 64 blocks is symmetric positive definite. `coarse_inverse`: symmetric positive definite.
All inputs are finite; a program needn't handle non-finite values.
Results may differ from a plain program's by a relative error of at most 0.00018.
Values sent between devices are 32-bit elements; how exact they have to be, the bound alone decides.
A program may use at most 64 MiB of HBM per device.

v0:
```python
import math
import jax
import jax.numpy as jnp
from jax import lax
from jax.sharding import PartitionSpec as P

NC = 32
ITERS = 2
NI = 128
highest = lax.Precision.HIGHEST
time_step = 0.5
newmark_beta = 0.25
newmark_gamma = 0.5


def shifted(array, axis, by):
    count = lax.axis_size(axis)
    return lax.ppermute(array, axis, [(i, (i + by) % count) for i in range(count)])


def contract(segment, matrix_rows):
    return lax.dot_general(segment, matrix_rows, (((1,), (1,)), ((), ())), precision=highest)


def shards(
    rr_inverse,
    corner_modes,
    coarse_inverse,
    inertia,
    disp_now,
    vel_now,
    acc_now,
    load_next,
    basis_rows,
    piece_owner,
):
    case_count, sub_count, unknowns = disp_now.shape
    coarse_total = coarse_inverse.shape[1]
    row_count = sub_count * NC
    shifted_rows = jnp.roll(coarse_inverse, NC, axis=1)
    coarse_pairs = jnp.concatenate(
        [
            shifted_rows.reshape(row_count, coarse_total // NC, NC),
            coarse_inverse.reshape(row_count, coarse_total // NC, NC),
        ],
        axis=2,
    ).reshape(row_count, 2 * coarse_total)

    def apply_green(field):
        local_part = jnp.einsum("jab,cjb->cja", rr_inverse, field, precision=highest)
        corner_terms = jnp.einsum("jmb,cjb->cjm", corner_modes, field, precision=highest)
        flat_terms = corner_terms.reshape(case_count, sub_count * 2 * NC)
        owned_sums = contract(
            lax.all_gather(flat_terms, ("sub", "grp"), axis=1, tiled=True), coarse_pairs
        )
        previous = shifted(owned_sums[:, row_count - NC :], ("sub", "grp"), 1)
        owned_blocks = owned_sums.reshape(case_count, sub_count, NC)
        left_values = jnp.concatenate(
            [previous.reshape(case_count, 1, NC), owned_blocks[:, :-1]], axis=1
        )
        coarse_values = jnp.concatenate([left_values, owned_blocks], axis=2)
        return local_part + jnp.einsum(
            "jmb,cjm->cjb", corner_modes, coarse_values, precision=highest
        )

    def interface_jump(field):
        following = shifted(field[:, :1, :NI], ("sub", "grp"), -1)
        first_parts = jnp.concatenate([field[:, 1:, :NI], following], axis=1)
        return field[:, :, unknowns - NI :] - first_parts

    def squared_norm(values):
        return lax.psum(jnp.sum(values * values, axis=(1, 2)), ("sub", "grp"))

    right_side = load_next + inertia[None] * (
        disp_now + time_step * vel_now + (0.5 - newmark_beta) * time_step * time_step * acc_now
    )
    green_rhs = apply_green(right_side)
    residual = interface_jump(green_rhs)
    carried = green_rhs
    direction = residual
    norm_now = squared_norm(residual)
    for iteration in range(ITERS):
        earlier = shifted(direction[:, -1:], ("sub", "grp"), 1)
        left_parts = jnp.concatenate([earlier, direction[:, :-1]], axis=1)
        middle = jnp.zeros((case_count, sub_count, unknowns - 2 * NI), jnp.float32)
        image_field = apply_green(jnp.concatenate([-left_parts, middle, direction], axis=2))
        image = interface_jump(image_field)
        curvature = lax.psum(jnp.sum(direction * image, axis=(1, 2)), ("sub", "grp"))
        alpha = (norm_now / curvature)[:, None, None]
        carried = carried - alpha * image_field
        residual = residual - alpha * image
        if iteration + 1 < ITERS:
            norm_next = squared_norm(residual)
            direction = residual + (norm_next / norm_now)[:, None, None] * direction
            norm_now = norm_next
    accel_new = (
        (carried - disp_now) / (newmark_beta * time_step * time_step)
        - vel_now / (newmark_beta * time_step)
        - (0.5 / newmark_beta - 1.0) * acc_now
    )
    vel_new = vel_now + time_step * ((1.0 - newmark_gamma) * acc_now + newmark_gamma * accel_new)
    piece_total = lax.axis_size(("sub", "grp"))
    piece_rows = unknowns // piece_total
    inverse = (
        jnp.zeros((piece_total,), jnp.int32)
        .at[piece_owner]
        .set(jnp.arange(piece_total, dtype=jnp.int32))
    )
    outgoing = carried.reshape(case_count, sub_count, piece_total, piece_rows)[:, :, inverse, :]
    outgoing = jnp.transpose(outgoing, (0, 2, 1, 3)).reshape(
        case_count, piece_total * sub_count * piece_rows
    )
    received = lax.all_to_all(outgoing, ("sub", "grp"), split_axis=1, concat_axis=1, tiled=True)
    projection_part = lax.dot_general(
        basis_rows, received, (((0,), (1,)), ((), ())), precision=highest
    )
    projection = lax.psum(projection_part, ("sub", "grp"))
    remainder = received - lax.dot_general(
        projection, basis_rows, (((0,), (1,)), ((), ())), precision=highest
    )
    gram_local = lax.dot_general(remainder, remainder, (((1,), (1,)), ((), ())), precision=highest)
    lower = jnp.linalg.cholesky(lax.psum(gram_local, ("sub", "grp")))
    scale_rows = math.sqrt(received.shape[1] * piece_total)
    new_columns = jax.scipy.linalg.solve_triangular(lower, remainder, lower=True) * scale_rows
    r_factor = lower.T / scale_rows
    return (carried, vel_new, projection, r_factor, new_columns)


def solution(mesh):
    return jax.shard_map(
        shards,
        mesh=mesh,
        in_specs=(
            P(("sub", "grp"), None, None),
            P(("sub", "grp"), None, None),
            P(("sub", "grp"), None),
            P(("sub", "grp"), None),
            P(None, ("sub", "grp"), None),
            P(None, ("sub", "grp"), None),
            P(None, ("sub", "grp"), None),
            P(None, ("sub", "grp"), None),
            P(("sub", "grp"), None),
            P(),
        ),
        out_specs=(
            P(None, ("sub", "grp"), None),
            P(None, ("sub", "grp"), None),
            P(),
            P(),
            P(None, ("sub", "grp")),
        ),
        check_vma=False,
    )
```

profile of v0, /device:TPU:0, one launch (start us, length us, event | category | flops | bytes accessed | tf_op | source)
XLA Modules:
  0.0 396.2 jit_solution(17063526511338648422)
XLA Ops:
  0.7 1.5 copy.65
  2.2 1.1 slice.101
  3.8 43.6 %all_gather.9 = f32[8,4096]{1,0:T(8,128)S(1)} all-gather(f32[8,128]{1,0:T(8,128)S(1)} %reshape.67), channel_id=1, replica_groups=mesh['sub'=8,'grp'=4] {'sub','grp'}, dimensions={1}, use_global_device_ids=true | all-gather | bytes 135168 | tf_op jit(solution)/shard_map/all_gather | solution.py:54
  47.4 1.3 pad_maximum_fusion.1
  48.9 1.3 copy-done.1
  50.2 1.1 fusion.49
  51.8 1.8 fusion.10
  53.7 4.4 %collective-permute-done = f32[8,32]{1,0:T(8,128)S(1)} collective-permute-done((f32[8,32]{1,0:T(8,128)S(1)}, f32[8,32]{1,0:T(8,128)S(1)}, u32[]{:S(2)}, u32[]{:S(2)}) %collective-permute-start) | collective-permute-done | bytes 1056 | tf_op jit(solution)/shard_map/ppermute | solution.py:18
  58.4 0.7 collective-permute-start.1
  59.0 1.3 collective-permute-done.1
  60.4 6.6 %collective-permute-done.2 = f32[8,1,128]{2,0,1:T(8,128)S(1)} collective-permute-done((f32[8,1,128]{2,0,1:T(8,128)S(1)}, f32[8,1,128]{2,0,1:T(8,128)S(1)}, u32[]{:S(2)}, u32[]{:S(2)}) %collective-permute-start.2) | collective-permute-done | bytes 4128 | tf_op jit(solution)/shard_map/ppermute | solution.py:18
  67.4 36.7 %all_gather.10 = f32[8,4096]{1,0:T(8,128)S(1)} all-gather(f32[8,128]{1,0:T(8,128)S(1)} %reshape.73), channel_id=1, replica_groups=mesh['sub'=8,'grp'=4] {'sub','grp'}, dimensions={1}, use_global_device_ids=true | all-gather | bytes 135168 | tf_op jit(solution)/shard_map/all_gather | solution.py:54
  104.1 2.7 fusion.50
  107.2 1.8 fusion.5
  109.1 4.4 %collective-permute-done.3 = f32[8,32]{1,0:T(8,128)S(1)} collective-permute-done((f32[8,32]{1,0:T(8,128)S(1)}, f32[8,32]{1,0:T(8,128)S(1)}, u32[]{:S(2)}, u32[]{:S(2)}) %collective-permute-start.3) | collective-permute-done | bytes 1056 | tf_op jit(solution)/shard_map/ppermute | solution.py:18
  113.8 0.7 collective-permute-start.4
  114.5 1.3 collective-permute-done.4
  116.0 38.1 %all-reduce = (f32[8]{0:T(128)S(1)}, f32[8]{0:T(128)S(1)}) all-reduce(f32[8]{0:T(128)S(1)} %get-tuple-element.21, f32[8]{0:T(128)S(1)} %get-tuple-element.20), channel_id=1, replica_groups=mesh['sub'=8,'grp'=4] {'sub','grp'}, use_global_device_ids=true, to_apply=%region_1.2 | all-reduce | flops 16 | bytes 128 | tf_op jit(solution)/shard_map/psum | solution.py:72
  154.3 42.1 %psum.44 = f32[8]{0:T(128)S(1)} all-reduce(f32[8]{0:T(128)S(1)} %multiply_reduce_fusion), channel_id=1, replica_groups=mesh['sub'=8,'grp'=4] {'sub','grp'}, use_global_device_ids=true, to_apply=%region_5.6 | all-reduce | flops 8 | bytes 64 | tf_op jit(solution)/shard_map/psum | solution.py:72
  196.5 0.7 scatter_custom_fusion
  197.2 5.9 %collective-permute-done.5 = f32[8,1,128]{2,0,1:T(8,128)S(1)} collective-permute-done((f32[8,1,128]{2,0,1:T(8,128)S(1)}, f32[8,1,128]{2,0,1:T(8,128)S(1)}, u32[]{:S(2)}, u32[]{:S(2)}) %collective-permute-start.5) | collective-permute-done | bytes 4128 | tf_op jit(solution)/shard_map/ppermute | solution.py:18
  203.5 36.7 %all_gather.11 = f32[8,4096]{1,0:T(8,128)S(1)} all-gather(f32[8,128]{1,0:T(8,128)S(1)} %reshape.76), channel_id=1, replica_groups=mesh['sub'=8,'grp'=4] {'sub','grp'}, dimensions={1}, use_global_device_ids=true | all-gather | bytes 135168 | tf_op jit(solution)/shard_map/all_gather | solution.py:54
  240.2 2.7 fusion.51
  242.9 0.5 collective-permute-start.6
  243.4 2.5 fusion.6
  246.0 3.7 collective-permute-done.6
  249.7 1.0 fusion
  250.8 1.4 collective-permute-start.7
  252.2 1.3 collective-permute-done.7
  253.6 38.1 %psum.45 = f32[8]{0:T(128)S(1)} all-reduce(f32[8]{0:T(128)S(1)} %fusion.17), channel_id=1, replica_groups=mesh['sub'=8,'grp'=4] {'sub','grp'}, use_global_device_ids=true, to_apply=%region_7.8 | all-reduce | flops 8 | bytes 64 | tf_op jit(solution)/shard_map/psum | solution.py:88
  291.7 1.5 fusion.4
  293.3 0.8 copy.81
  294.2 1.5 gather_fusion
  296.0 0.7 reshape.100
  296.7 6.5 %all-to-all-start = ((f32[32,1,256]{2,1,0:T(1,128)}), f32[32,1,256]{2,1,0:T(1,128)S(1)}, u32[]{:S(2)}, u32[]{:S(2)}) async-start(f32[32,1,256]{2,1,0:T(1,128)} %reshape.100), calls=%async_computation | async-start | bytes 65536 | tf_op jit(solution)/shard_map/all_to_all | solution.py:113
  303.2 1.4 copy.88
  304.6 1.4 copy.89
  306.0 4.5 %all-to-all-done = f32[32,1,256]{2,1,0:T(1,128)S(1)} async-done(((f32[32,1,256]{2,1,0:T(1,128)}), f32[32,1,256]{2,1,0:T(1,128)S(1)}, u32[]{:S(2)}, u32[]{:S(2)}) %all-to-all-start) | async-done | bytes 32800 | tf_op jit(solution)/shard_map/all_to_all | solution.py:113
  311.0 0.7 reduce.6
  312.5 38.3 %psum.46 = f32[256,8]{0,1:T(8,128)S(1)} all-reduce(f32[256,8]{0,1:T(8,128)S(1)} %convolution_bitcast_fusion), channel_id=1, replica_groups=mesh['sub'=8,'grp'=4] {'sub','grp'}, use_global_device_ids=true, to_apply=%region_9.10 | all-reduce | flops 2048 | bytes 16384 | tf_op jit(solution)/shard_map/psum | solution.py:117
  350.7 1.0 convolution_subtract_fusion
  351.8 40.1 %psum.47 = f32[8,8]{0,1:T(8,128)S(1)} all-reduce(f32[8,8]{0,1:T(8,128)S(1)} %fusion.52), channel_id=1, replica_groups=mesh['sub'=8,'grp'=4] {'sub','grp'}, use_global_device_ids=true, to_apply=%region_10.11 | all-reduce | flops 64 | bytes 512 | tf_op jit(solution)/shard_map/psum | solution.py:122
  392.0 0.7 cholesky.18
  392.7 0.6 compare_reduce_fusion
  393.4 0.6 select_bitcast_fusion
  394.0 0.6 custom-call.7
  394.7 0.9 convolution_multiply_fusion
  395.5 0.7 copy.90
  (86 shorter events, 5.8 us)
Async XLA Ops:
  0.6 51.1 %copy-start = (f32[2,512,512]{2,1,0:T(8,128)S(1)}, f32[2,512,512]{2,1,0:T(8,128)}, u32[]{:S(2)}) copy-start(f32[2,512,512]{2,1,0:T(8,128)} %param.10) | copy-start | bytes 6291460
  0.6 2.7 copy-start.6
  0.7 2.7 copy-start.7
  0.7 2.6 copy-start.5
  0.7 2.7 copy-start.2
  2.2 1.1 copy-start.9
  2.2 1.1 copy-start.10
  48.9 1.4 copy-start.1
  51.4 6.7 %collective-permute-start = (f32[8,32]{1,0:T(8,128)S(1)}, f32[8,32]{1,0:T(8,128)S(1)}, u32[]{:S(2)}, u32[]{:S(2)}) collective-permute-start(f32[8,32]{1,0:T(8,128)S(1)} %slice.79), channel_id=1, source_target_pairs={{0,1},{1,2},{2,3},{3,4},{4,5},{5,6},{6,7},{7,8},{8,9},{9,10},{10,1... | collective-permute-start | bytes 3080 | tf_op jit(solution)/shard_map/ppermute | solution.py:18
  58.4 2.0 collective-permute-start.1
  60.4 6.6 %collective-permute-start.2 = (f32[8,1,128]{2,0,1:T(8,128)S(1)}, f32[8,1,128]{2,0,1:T(8,128)S(1)}, u32[]{:S(2)}, u32[]{:S(2)}) collective-permute-start(f32[8,1,128]{2,0,1:T(8,128)S(1)} %get-tuple-element.34), channel_id=1, source_target_pairs={{0,1},{1,2},{2,3},{3,4},{4,5},{5,6},{6,7},{7,8},{8,9},{9,10},{10,1... | collective-permute-start | bytes 12296 | tf_op jit(solution)/shard_map/ppermute | solution.py:18
  104.1 92.4 %copy-start.11 = (s32[32]{0:T(128)S(1)}, s32[32]{0:T(128)}, u32[]{:S(2)}) copy-start(s32[32]{0:T(128)} %param.19) | copy-start | bytes 388
  106.9 6.6 %collective-permute-start.3 = (f32[8,32]{1,0:T(8,128)S(1)}, f32[8,32]{1,0:T(8,128)S(1)}, u32[]{:S(2)}, u32[]{:S(2)}) collective-permute-start(f32[8,32]{1,0:T(8,128)S(1)} %slice.86), channel_id=1, source_target_pairs={{0,1},{1,2},{2,3},{3,4},{4,5},{5,6},{6,7},{7,8},{8,9},{9,10},{10,1... | collective-permute-start | bytes 3080 | tf_op jit(solution)/shard_map/ppermute | solution.py:18
  113.8 2.0 collective-permute-start.4
  196.4 6.6 %collective-permute-start.5 = (f32[8,1,128]{2,0,1:T(8,128)S(1)}, f32[8,1,128]{2,0,1:T(8,128)S(1)}, u32[]{:S(2)}, u32[]{:S(2)}) collective-permute-start(f32[8,1,128]{2,0,1:T(8,128)S(1)} %get-tuple-element.32), channel_id=1, source_target_pairs={{0,1},{1,2},{2,3},{3,4},{4,5},{5,6},{6,7},{7,8},{8,9},{9,10},{10,1... | collective-permute-start | bytes 12296 | tf_op jit(solution)/shard_map/ppermute | solution.py:18
  242.9 6.8 %collective-permute-start.6 = (f32[8,32]{1,0:T(8,128)S(1)}, f32[8,32]{1,0:T(8,128)S(1)}, u32[]{:S(2)}, u32[]{:S(2)}) collective-permute-start(f32[8,32]{1,0:T(8,128)S(1)} %slice.93), channel_id=1, source_target_pairs={{0,1},{1,2},{2,3},{3,4},{4,5},{5,6},{6,7},{7,8},{8,9},{9,10},{10,1... | collective-permute-start | bytes 3080 | tf_op jit(solution)/shard_map/ppermute | solution.py:18
  245.9 66.0 %copy-start.3 = (f32[1024,256]{1,0:T(8,128)S(1)}, f32[1024,256]{1,0:T(8,128)}, u32[]{:S(2)}) copy-start(f32[1024,256]{1,0:T(8,128)} %param.18) | copy-start | bytes 3145732
  250.8 2.7 collective-permute-start.7
  293.2 2.5 copy-start.4
  296.7 13.7 %all-to-all-start = ((f32[32,1,256]{2,1,0:T(1,128)}), f32[32,1,256]{2,1,0:T(1,128)S(1)}, u32[]{:S(2)}, u32[]{:S(2)}) async-start(f32[32,1,256]{2,1,0:T(1,128)} %reshape.100), calls=%async_computation | async-start | bytes 65536 | tf_op jit(solution)/shard_map/all_to_all | solution.py:113
  350.7 45.5 %copy-start.8 = (f32[256,8]{0,1:T(8,128)}, f32[256,8]{0,1:T(8,128)S(1)}, u32[]{:S(2)}) copy-start(f32[256,8]{0,1:T(8,128)S(1)} %psum.46) | copy-start | bytes 24580
where the time goes:
time: 397 us; the launch traced here: 396 us
  blocking collectives  314 us (79%)
  waiting for transfers between devices  33.4 us (8%)
  matrix products  17.6 us (4%)
  local copies, waits for them, and re-layouts  13.2 us (3%)
  starting transfers between devices  10.5 us (3%)
  other arithmetic  6.97 us (2%)
    all_gather x3, blocking collectives, apply_green(): lax.all_gather(flat_terms, ('sub', 'grp'), axis=1, tiled=True)  117 us
    psum x2, blocking collectives, squared_norm(): return lax.psum(jnp.sum(values * values, axis=(1, 2)), ('sub', 'grp'))  80.2 us
    psum x1, blocking collectives, shards(): lower = jnp.linalg.cholesky(lax.psum(gram_local, ('sub', 'grp')))  40.1 us
    psum x1, blocking collectives, shards(): projection = lax.psum(projection_part, ('sub', 'grp'))  38.3 us
    psum x1, blocking collectives, shards(): lax.psum(jnp.sum(direction * image, axis=(1, 2)), ('sub', 'grp'))  38.1 us
    ppermute x8, waiting for transfers between devices, shifted(): lax.ppermute(array, axis, [(i, (i + by) % count) for i in range(count)])  29 us
  transfers between devices with their start and end apart: 9, of which 9 were waited for; matrix products, arithmetic and copies ran while one was open for 2% of the time, Pallas kernels for 0%

commit v1 on v0

--- a/solution.py
+++ b/solution.py
@@ -51,7 +51,7 @@
         corner_terms = jnp.einsum("jmb,cjb->cjm", corner_modes, field, precision=highest)
         flat_terms = corner_terms.reshape(case_count, sub_count * 2 * NC)
         owned_sums = contract(
-            lax.all_gather(flat_terms, ("sub", "grp"), axis=1, tiled=True), coarse_pairs
+            jnp.concatenate(lax.all_gather(flat_terms, ("sub", "grp")), axis=1), coarse_pairs
         )
         previous = shifted(owned_sums[:, row_count - NC :], ("sub", "grp"), 1)
         owned_blocks = owned_sums.reshape(case_count, sub_count, NC)

time: 397 us -> 397 us (level)
  no operation moved by 1% of the time
where the time goes in v1:
time: 397 us; the launch traced here: 396 us
  blocking collectives  314 us (79%)
  waiting for transfers between devices  33.4 us (8%)
  matrix products  17.6 us (4%)
  local copies, waits for them, and re-layouts  13.2 us (3%)
  starting transfers between devices  10.5 us (3%)
  other arithmetic  6.97 us (2%)
    all_gather x3, blocking collectives, apply_green(): lax.all_gather(flat_terms, ('sub', 'grp'))  117 us
    psum x2, blocking collectives, squared_norm(): return lax.psum(jnp.sum(values * values, axis=(1, 2)), ('sub', 'grp'))  80.2 us
    psum x1, blocking collectives, shards(): lower = jnp.linalg.cholesky(lax.psum(gram_local, ('sub', 'grp')))  40.1 us
    psum x1, blocking collectives, shards(): projection = lax.psum(projection_part, ('sub', 'grp'))  38.3 us
    psum x1, blocking collectives, shards(): lax.psum(jnp.sum(direction * image, axis=(1, 2)), ('sub', 'grp'))  38.1 us
    ppermute x8, waiting for transfers between devices, shifted(): lax.ppermute(array, axis, [(i, (i + by) % count) for i in range(count)])  29 us
  transfers between devices with their start and end apart: 9, of which 9 were waited for; matrix products, arithmetic and copies ran while one was open for 2% of the time, Pallas kernels for 0%

profile of v1, /device:TPU:0, one launch (start us, length us, event | category | flops | bytes accessed | tf_op | source)
XLA Modules:
  0.0 396.2 jit_solution(15051737813497982045)
XLA Ops:
  0.7 1.5 copy.65
  2.2 1.1 slice.101
  3.8 43.6 %all_gather.9 = f32[32,8,128]{2,1,0:T(8,128)S(1)} all-gather(f32[1,8,128]{2,1,0:T(8,128)S(1)} %all_gather_reshape.9), channel_id=1, replica_groups=mesh['sub'=8,'grp'=4] {'sub','grp'}, dimensions={0}, use_global_device_ids=true | all-gather | bytes 135168 | tf_op jit(solution)/shard_map/all_gather | solution.py:54
  47.4 1.3 pad_maximum_fusion.1
  48.9 1.3 copy-done.1
  50.2 1.1 fusion.7
  51.8 1.8 fusion.16
  53.7 4.4 %collective-permute-done = f32[8,32]{1,0:T(8,128)S(1)} collective-permute-done((f32[8,32]{1,0:T(8,128)S(1)}, f32[8,32]{1,0:T(8,128)S(1)}, u32[]{:S(2)}, u32[]{:S(2)}) %collective-permute-start) | collective-permute-done | bytes 1056 | tf_op jit(solution)/shard_map/ppermute | solution.py:18
  58.4 0.7 collective-permute-start.1
  59.0 1.3 collective-permute-done.1
  60.4 6.6 %collective-permute-done.2 = f32[8,1,128]{2,0,1:T(8,128)S(1)} collective-permute-done((f32[8,1,128]{2,0,1:T(8,128)S(1)}, f32[8,1,128]{2,0,1:T(8,128)S(1)}, u32[]{:S(2)}, u32[]{:S(2)}) %collective-permute-start.2) | collective-permute-done | bytes 4128 | tf_op jit(solution)/shard_map/ppermute | solution.py:18
  67.4 36.7 %all_gather.10 = f32[32,8,128]{2,1,0:T(8,128)S(1)} all-gather(f32[1,8,128]{2,1,0:T(8,128)S(1)} %all_gather_reshape.10), channel_id=1, replica_groups=mesh['sub'=8,'grp'=4] {'sub','grp'}, dimensions={0}, use_global_device_ids=true | all-gather | bytes 135168 | tf_op jit(solution)/shard_map/all_gather | solution.py:54
  104.1 2.7 fusion.5
  107.2 1.8 fusion.11
  109.1 4.4 %collective-permute-done.3 = f32[8,32]{1,0:T(8,128)S(1)} collective-permute-done((f32[8,32]{1,0:T(8,128)S(1)}, f32[8,32]{1,0:T(8,128)S(1)}, u32[]{:S(2)}, u32[]{:S(2)}) %collective-permute-start.3) | collective-permute-done | bytes 1056 | tf_op jit(solution)/shard_map/ppermute | solution.py:18
  113.8 0.7 collective-permute-start.4
  114.5 1.3 collective-permute-done.4
  116.0 38.1 %all-reduce = (f32[8]{0:T(128)S(1)}, f32[8]{0:T(128)S(1)}) all-reduce(f32[8]{0:T(128)S(1)} %get-tuple-element.21, f32[8]{0:T(128)S(1)} %get-tuple-element.20), channel_id=1, replica_groups=mesh['sub'=8,'grp'=4] {'sub','grp'}, use_global_device_ids=true, to_apply=%region_1.2 | all-reduce | flops 16 | bytes 128 | tf_op jit(solution)/shard_map/psum | solution.py:72
  154.3 42.1 %psum.44 = f32[8]{0:T(128)S(1)} all-reduce(f32[8]{0:T(128)S(1)} %multiply_reduce_fusion), channel_id=1, replica_groups=mesh['sub'=8,'grp'=4] {'sub','grp'}, use_global_device_ids=true, to_apply=%region_5.6 | all-reduce | flops 8 | bytes 64 | tf_op jit(solution)/shard_map/psum | solution.py:72
  196.5 0.7 scatter_custom_fusion
  197.2 5.9 %collective-permute-done.5 = f32[8,1,128]{2,0,1:T(8,128)S(1)} collective-permute-done((f32[8,1,128]{2,0,1:T(8,128)S(1)}, f32[8,1,128]{2,0,1:T(8,128)S(1)}, u32[]{:S(2)}, u32[]{:S(2)}) %collective-permute-start.5) | collective-permute-done | bytes 4128 | tf_op jit(solution)/shard_map/ppermute | solution.py:18
  203.5 36.7 %all_gather.11 = f32[32,8,128]{2,1,0:T(8,128)S(1)} all-gather(f32[1,8,128]{2,1,0:T(8,128)S(1)} %all_gather_reshape.11), channel_id=1, replica_groups=mesh['sub'=8,'grp'=4] {'sub','grp'}, dimensions={0}, use_global_device_ids=true | all-gather | bytes 135168 | tf_op jit(solution)/shard_map/all_gather | solution.py:54
  240.2 2.7 fusion.3
  242.9 0.5 collective-permute-start.6
  243.4 2.5 fusion.12
  246.0 3.7 collective-permute-done.6
  249.7 1.0 fusion
  250.8 1.4 collective-permute-start.7
  252.2 1.3 collective-permute-done.7
  253.6 38.1 %psum.45 = f32[8]{0:T(128)S(1)} all-reduce(f32[8]{0:T(128)S(1)} %fusion.23), channel_id=1, replica_groups=mesh['sub'=8,'grp'=4] {'sub','grp'}, use_global_device_ids=true, to_apply=%region_7.8 | all-reduce | flops 8 | bytes 64 | tf_op jit(solution)/shard_map/psum | solution.py:88
  291.7 1.5 fusion.10
  293.3 0.8 copy.81
  294.2 1.5 gather_fusion
  296.0 0.7 reshape.112
  296.7 6.5 %all-to-all-start = ((f32[32,1,256]{2,1,0:T(1,128)}), f32[32,1,256]{2,1,0:T(1,128)S(1)}, u32[]{:S(2)}, u32[]{:S(2)}) async-start(f32[32,1,256]{2,1,0:T(1,128)} %reshape.112), calls=%async_computation | async-start | bytes 65536 | tf_op jit(solution)/shard_map/all_to_all | solution.py:113
  303.2 1.4 copy.88
  304.6 1.4 copy.89
  306.0 4.5 %all-to-all-done = f32[32,1,256]{2,1,0:T(1,128)S(1)} async-done(((f32[32,1,256]{2,1,0:T(1,128)}), f32[32,1,256]{2,1,0:T(1,128)S(1)}, u32[]{:S(2)}, u32[]{:S(2)}) %all-to-all-start) | async-done | bytes 32800 | tf_op jit(solution)/shard_map/all_to_all | solution.py:113
  311.0 0.7 reduce.6
  312.5 38.3 %psum.46 = f32[256,8]{0,1:T(8,128)S(1)} all-reduce(f32[256,8]{0,1:T(8,128)S(1)} %convolution_bitcast_fusion), channel_id=1, replica_groups=mesh['sub'=8,'grp'=4] {'sub','grp'}, use_global_device_ids=true, to_apply=%region_9.10 | all-reduce | flops 2048 | bytes 16384 | tf_op jit(solution)/shard_map/psum | solution.py:117
  350.7 1.0 convolution_subtract_fusion
  351.8 40.1 %psum.47 = f32[8,8]{0,1:T(8,128)S(1)} all-reduce(f32[8,8]{0,1:T(8,128)S(1)} %fusion.55), channel_id=1, replica_groups=mesh['sub'=8,'grp'=4] {'sub','grp'}, use_global_device_ids=true, to_apply=%region_10.11 | all-reduce | flops 64 | bytes 512 | tf_op jit(solution)/shard_map/psum | solution.py:122
  392.0 0.7 cholesky.18
  392.7 0.6 compare_reduce_fusion
  393.4 0.6 select_bitcast_fusion
  394.0 0.6 custom-call.7
  394.7 0.9 convolution_multiply_fusion
  395.5 0.7 copy.90
  (86 shorter events, 5.8 us)
Async XLA Ops:
  0.6 51.1 %copy-start = (f32[2,512,512]{2,1,0:T(8,128)S(1)}, f32[2,512,512]{2,1,0:T(8,128)}, u32[]{:S(2)}) copy-start(f32[2,512,512]{2,1,0:T(8,128)} %param.10) | copy-start | bytes 6291460
  0.6 2.7 copy-start.6
  0.7 2.7 copy-start.7
  0.7 2.6 copy-start.5
  0.7 2.7 copy-start.2
  2.2 1.1 copy-start.9
  2.2 1.1 copy-start.10
  48.9 1.4 copy-start.1
  51.4 6.7 %collective-permute-start = (f32[8,32]{1,0:T(8,128)S(1)}, f32[8,32]{1,0:T(8,128)S(1)}, u32[]{:S(2)}, u32[]{:S(2)}) collective-permute-start(f32[8,32]{1,0:T(8,128)S(1)} %slice.79), channel_id=1, source_target_pairs={{0,1},{1,2},{2,3},{3,4},{4,5},{5,6},{6,7},{7,8},{8,9},{9,10},{10,1... | collective-permute-start | bytes 3080 | tf_op jit(solution)/shard_map/ppermute | solution.py:18
  58.4 2.0 collective-permute-start.1
  60.4 6.6 %collective-permute-start.2 = (f32[8,1,128]{2,0,1:T(8,128)S(1)}, f32[8,1,128]{2,0,1:T(8,128)S(1)}, u32[]{:S(2)}, u32[]{:S(2)}) collective-permute-start(f32[8,1,128]{2,0,1:T(8,128)S(1)} %get-tuple-element.34), channel_id=1, source_target_pairs={{0,1},{1,2},{2,3},{3,4},{4,5},{5,6},{6,7},{7,8},{8,9},{9,10},{10,1... | collective-permute-start | bytes 12296 | tf_op jit(solution)/shard_map/ppermute | solution.py:18
  104.1 92.4 %copy-start.11 = (s32[32]{0:T(128)S(1)}, s32[32]{0:T(128)}, u32[]{:S(2)}) copy-start(s32[32]{0:T(128)} %param.19) | copy-start | bytes 388
  106.9 6.6 %collective-permute-start.3 = (f32[8,32]{1,0:T(8,128)S(1)}, f32[8,32]{1,0:T(8,128)S(1)}, u32[]{:S(2)}, u32[]{:S(2)}) collective-permute-start(f32[8,32]{1,0:T(8,128)S(1)} %slice.86), channel_id=1, source_target_pairs={{0,1},{1,2},{2,3},{3,4},{4,5},{5,6},{6,7},{7,8},{8,9},{9,10},{10,1... | collective-permute-start | bytes 3080 | tf_op jit(solution)/shard_map/ppermute | solution.py:18
  113.8 2.0 collective-permute-start.4
  196.4 6.6 %collective-permute-start.5 = (f32[8,1,128]{2,0,1:T(8,128)S(1)}, f32[8,1,128]{2,0,1:T(8,128)S(1)}, u32[]{:S(2)}, u32[]{:S(2)}) collective-permute-start(f32[8,1,128]{2,0,1:T(8,128)S(1)} %get-tuple-element.32), channel_id=1, source_target_pairs={{0,1},{1,2},{2,3},{3,4},{4,5},{5,6},{6,7},{7,8},{8,9},{9,10},{10,1... | collective-permute-start | bytes 12296 | tf_op jit(solution)/shard_map/ppermute | solution.py:18
  242.9 6.8 %collective-permute-start.6 = (f32[8,32]{1,0:T(8,128)S(1)}, f32[8,32]{1,0:T(8,128)S(1)}, u32[]{:S(2)}, u32[]{:S(2)}) collective-permute-start(f32[8,32]{1,0:T(8,128)S(1)} %slice.93), channel_id=1, source_target_pairs={{0,1},{1,2},{2,3},{3,4},{4,5},{5,6},{6,7},{7,8},{8,9},{9,10},{10,1... | collective-permute-start | bytes 3080 | tf_op jit(solution)/shard_map/ppermute | solution.py:18
  245.9 66.0 %copy-start.3 = (f32[1024,256]{1,0:T(8,128)S(1)}, f32[1024,256]{1,0:T(8,128)}, u32[]{:S(2)}) copy-start(f32[1024,256]{1,0:T(8,128)} %param.18) | copy-start | bytes 3145732
  250.8 2.7 collective-permute-start.7
  293.2 2.5 copy-start.4
  296.7 13.7 %all-to-all-start = ((f32[32,1,256]{2,1,0:T(1,128)}), f32[32,1,256]{2,1,0:T(1,128)S(1)}, u32[]{:S(2)}, u32[]{:S(2)}) async-start(f32[32,1,256]{2,1,0:T(1,128)} %reshape.112), calls=%async_computation | async-start | bytes 65536 | tf_op jit(solution)/shard_map/all_to_all | solution.py:113
  350.7 45.5 %copy-start.8 = (f32[256,8]{0,1:T(8,128)}, f32[256,8]{0,1:T(8,128)S(1)}, u32[]{:S(2)}) copy-start(f32[256,8]{0,1:T(8,128)S(1)} %psum.46) | copy-start | bytes 24580
